TPU v7x, 32 devices: a whole 2x2x4 slice. The times are simulated.
32 devices in a mesh: section: 4 (over z), dp: 8 (over y, x, core).
Axes of the slice: x: 2, y: 2, z: 4, core: 2. Of those that a mesh axis runs over, the one named last changes fastest.
Arguments:
- stream: float32 [2, 64, 16, 16, 128], P(None, 'dp'), may hold values from -6 to 6
- cotangent: float32 [2, 64, 16, 16, 128], P(None, 'dp'), may hold values from -6 to 6
- weights: bfloat16 [4, 2304, 128], P('section'), may hold values from -0.09375 to 0.09375
- master: float32 [4, 2304, 128], P('section', 'dp'), may hold values from -0.09375 to 0.09375
- momentum: float32 [4, 2304, 128], P('section', 'dp'), may hold values from -6 to 6
Outputs:
- new_master: float32 [4, 2304, 128], P('section', 'dp')
- new_momentum: float32 [4, 2304, 128], P('section', 'dp')
- new_weights: bfloat16 [4, 2304, 128], P('section')
All inputs are finite; a program needn't handle non-finite values.
Results may differ from a plain program's by a relative error of at most 0.014.
Values may be sent and summed in bfloat16 or wider, within the bound.
A program may use at most 64 MiB of HBM per device.

v0:
```python
import jax
import jax.numpy as jnp
from jax import lax
from jax.sharding import PartitionSpec as P

LAYERS = 1
step_size = 0.1
inertia = 0.9


def columns(field):
    height = field.shape[1]
    breadth = field.shape[2]
    padded = jnp.pad(jax.nn.silu(field).astype(jnp.bfloat16), ((0, 0), (1, 1), (1, 1), (0, 0)))
    shifted = [
        padded[:, row_tap : row_tap + height, col_tap : col_tap + breadth, :]
        for row_tap in range(3)
        for col_tap in range(3)
    ]
    return jnp.concatenate(shifted, axis=3).reshape(-1, 9 * field.shape[3])


def convolve(patches, weight, template):
    return jnp.dot(patches, weight, preferred_element_type=jnp.float32).reshape(template.shape)


def spread(rounded, weight, template):
    height, breadth, channels = (template.shape[1], template.shape[2], template.shape[3])
    spread_cols = lax.dot_general(
        rounded, weight, (((1,), (1,)), ((), ())), preferred_element_type=jnp.float32
    )
    spread_cols = spread_cols.reshape(template.shape[0], height, breadth, 9 * channels)
    padded = jnp.pad(spread_cols, ((0, 0), (1, 1), (1, 1), (0, 0)))
    summed = jnp.zeros(template.shape, jnp.float32)
    for row_tap in range(3):
        for col_tap in range(3):
            tap_index = 3 * row_tap + col_tap
            summed = (
                summed
                + padded[
                    :,
                    2 - row_tap : 2 - row_tap + height,
                    2 - col_tap : 2 - col_tap + breadth,
                    tap_index * channels : (tap_index + 1) * channels,
                ]
            )
    return summed


def weight_grad(patches, rounded):
    return lax.dot_general(
        patches, rounded, (((0,), (0,)), ((), ())), preferred_element_type=jnp.float32
    )


def silu_slope(field):
    logistic = jax.nn.sigmoid(field)
    return logistic * (1.0 + field * (1.0 - logistic))


def coupling_forward(first, second, weight_f, weight_g):
    patch_f = columns(second)
    out_first = first + convolve(patch_f, weight_f, second)
    patch_g = columns(out_first)
    out_second = second + convolve(patch_g, weight_g, out_first)
    return (out_first, out_second, patch_f, patch_g)


def coupling_grads(
    patch_f, second, patch_g, out_first, grad_first, grad_second, weight_f, weight_g
):
    channels = out_first.shape[3]
    round_second = grad_second.astype(jnp.bfloat16).reshape(-1, channels)
    wgrad_g = weight_grad(patch_g, round_second)
    grad_first = grad_first + spread(round_second, weight_g, out_first) * silu_slope(out_first)
    round_first = grad_first.astype(jnp.bfloat16).reshape(-1, channels)
    wgrad_f = weight_grad(patch_f, round_first)
    grad_second = grad_second + spread(round_first, weight_f, second) * silu_slope(second)
    return (grad_first, grad_second, wgrad_f, wgrad_g)


def coupling_backward(out_first, out_second, grad_first, grad_second, weight_f, weight_g):
    patch_g = columns(out_first)
    second = out_second - convolve(patch_g, weight_g, out_first)
    patch_f = columns(second)
    first = out_first - convolve(patch_f, weight_f, second)
    grad_first, grad_second, wgrad_f, wgrad_g = coupling_grads(
        patch_f, second, patch_g, out_first, grad_first, grad_second, weight_f, weight_g
    )
    return (first, second, grad_first, grad_second, wgrad_f, wgrad_g)


def replicated_grads(stream, cotangent, weights):
    section_index = lax.axis_index("section")
    sections = lax.axis_size("section")
    channels = weights.shape[2]
    gathered = lax.all_gather(weights, "section", axis=0, tiled=True)
    all_blocks = gathered.reshape(sections, LAYERS, 2, 9 * channels, channels)
    share = stream.shape[1] // sections
    own = lax.dynamic_slice_in_dim(stream, section_index * share, share, 1)
    seed = lax.dynamic_slice_in_dim(cotangent, section_index * share, share, 1)

    def forward_one(section_idx, pair):
        blocks = lax.dynamic_index_in_dim(all_blocks, section_idx, 0, keepdims=False)
        first, second = pair
        first, second, patch_f, patch_g = coupling_forward(
            first, second, blocks[0, 0], blocks[0, 1]
        )
        return (first, second)

    first, second = lax.fori_loop(0, sections, forward_one, (own[0], own[1]))

    def backward_one(turn, carry):
        out_first, out_second, grad_first, grad_second, grads = carry
        section_idx = sections - 1 - turn
        blocks = lax.dynamic_index_in_dim(all_blocks, section_idx, 0, keepdims=False)
        pieces = []
        for coupling in reversed(range(LAYERS)):
            out_first, out_second, grad_first, grad_second, wgrad_f, wgrad_g = coupling_backward(
                out_first,
                out_second,
                grad_first,
                grad_second,
                blocks[coupling, 0],
                blocks[coupling, 1],
            )
            pieces.append(jnp.stack([wgrad_f, wgrad_g]))
        pieces = pieces[::-1]
        grads = lax.dynamic_update_index_in_dim(grads, jnp.stack(pieces), section_idx, 0)
        return (out_first, out_second, grad_first, grad_second, grads)

    grads_zero = jnp.zeros((sections, LAYERS, 2, 9 * channels, channels), jnp.float32)
    result = lax.fori_loop(0, sections, backward_one, (first, second, seed[0], seed[1], grads_zero))
    return lax.psum_scatter(
        result[4].reshape(-1, channels), ("section", "dp"), scatter_dimension=0, tiled=True
    )


def on_device(stream, cotangent, weights, master, momentum):
    summed = replicated_grads(stream, cotangent, weights)
    images = stream.shape[1] * lax.axis_size("dp")
    gradient = summed / images
    new_momentum = inertia * momentum[0] + gradient
    new_master = master[0] - step_size * new_momentum
    new_weights = lax.all_gather(new_master.astype(jnp.bfloat16), "dp", axis=0, tiled=True)
    return (new_master[None], new_momentum[None], new_weights[None])


def solution(mesh):
    placed = (
        P(None, "dp", None, None, None),
        P(None, "dp", None, None, None),
        P("section", None, None),
        P("section", "dp", None),
        P("section", "dp", None),
    )
    return jax.shard_map(
        on_device,
        mesh=mesh,
        in_specs=placed,
        out_specs=(P("section", "dp", None), P("section", "dp", None), P("section", None, None)),
        check_vma=False,
    )
```

profile of v0, /device:TPU:0, one launch (start us, length us, event | category | flops | bytes accessed | tf_op | source)
XLA Modules:
  0.0 230.6 jit_solution(14302645406688901209)
XLA Ops:
  7.2 0.7 all-gather.2.cloned.1.call-update
  7.9 1.3 dynamic-slice_bitcast_fusion.2
  9.2 53.1 %all-gather.2.cloned.1.call-done = bf16[4,2304,128]{2,1,0:T(8,128)(2,1)} async-done(((bf16[1,2304,128]{2,1,0:T(8,128)(2,1)}), bf16[4,2304,128]{2,1,0:T(8,128)(2,1)}) %all-gather.2.cloned.1.call-update) | async-done | bytes 2359312 | tf_op jit(solution)/shard_map/all_gather | solution.py:97
  62.3 13.1 %while.40 = (s32[]{:T(128)}, f32[2,16,16,128]{3,2,1,0:T(8,128)S(1)}, f32[2,16,16,128]{3,2,1,0:T(8,128)S(1)}, bf16[4,1,2,1152,128]{4,3,2,1,0:T(8,128)(2,1)}, s32[]{:T(128)}) while((s32[]{:T(128)}, f32[2,16,16,128]{3,2,1,0:T(8,128)S(1)}, f32[2,16,16,128]{3,2,1,0:T(8,128)S(1)}, bf16[4,1,2,1152,128]{4,3,2,1,0:T(8,128)(2,1)}, s32[]{:T(128)}) %tuple.101), condition=%wide.region_1.2_spmd, body=%wide.region_0.1_spmd.sunk | while | flops 303104000 | bytes 10551369 | solution.py:111
  62.4 1.1 dynamic-slice_bitcast_fusion.8
  63.7 0.1 constant_dynamic-update-slice_fusion.8
  64.0 0.6 multiply_convert_fusion.7
  65.0 0.5 convolution_add_fusion.3
  65.6 1.1 dynamic-slice_bitcast_fusion.8
  67.0 0.1 constant_dynamic-update-slice_fusion.8
  67.3 0.6 multiply_convert_fusion.7
  68.3 0.5 convolution_add_fusion.3
  68.8 0.1 multiply_convert_fusion.6
  68.9 1.1 dynamic-slice_bitcast_fusion.8
  70.2 0.1 constant_dynamic-update-slice_fusion.8
  70.6 0.6 multiply_convert_fusion.7
  71.6 0.5 convolution_add_fusion.3
  72.1 0.1 multiply_convert_fusion.6
  72.2 1.1 dynamic-slice_bitcast_fusion.8
  73.5 0.1 constant_dynamic-update-slice_fusion.8
  73.8 0.6 multiply_convert_fusion.7
  74.9 0.5 convolution_add_fusion.3
  75.4 2.5 %broadcast_in_dim.23 = f32[4,1,2,1152,128]{4,3,2,1,0:T(8,128)} broadcast(f32[]{:T(128)} %constant.135.clone.1), dimensions={} | broadcast | bytes 4718596 | tf_op jit(solution)/shard_map/broadcast_in_dim | solution.py:132
  77.9 27.0 %while.41 = (s32[]{:T(128)}, f32[2,16,16,128]{3,2,1,0:T(8,128)S(1)}, f32[2,16,16,128]{3,2,1,0:T(8,128)S(1)}, f32[2,16,16,128]{3,2,1,0:T(8,128)S(1)}, f32[2,16,16...) while((s32[]{:T(128)}, ...), condition=%wide.region_3.4_spmd, body=%wide.region_2.3_spmd.sunk | while | flops 909082624 | bytes 29098156 | solution.py:133
  77.9 1.1 dynamic-slice_bitcast_fusion.9
  79.0 0.5 fusion.147
  79.5 0.3 fusion.148
  80.3 0.5 convolution_bitcast_fusion.4
  80.8 0.5 fusion.149
  81.3 0.7 fusion.158
  82.5 0.5 convolution_subtract_fusion.3
  83.0 0.5 convolution_bitcast_fusion.5
  83.5 1.1 fusion.167
  84.7 1.1 dynamic-slice_bitcast_fusion.9
  85.8 0.5 fusion.147
  86.3 0.3 fusion.148
  87.1 0.5 convolution_bitcast_fusion.4
  87.6 0.5 fusion.149
  88.1 0.7 fusion.158
  89.3 0.5 convolution_subtract_fusion.3
  89.8 0.5 convolution_bitcast_fusion.5
  90.3 1.1 fusion.167
  91.4 1.1 dynamic-slice_bitcast_fusion.9
  92.5 0.5 fusion.147
  93.0 0.3 fusion.148
  93.8 0.5 convolution_bitcast_fusion.4
  94.3 0.5 fusion.149
  94.8 0.7 fusion.158
  96.0 0.5 convolution_subtract_fusion.3
  96.5 0.5 convolution_bitcast_fusion.5
  97.0 1.1 fusion.167
  98.2 1.1 dynamic-slice_bitcast_fusion.9
  99.3 0.5 fusion.147
  99.7 0.3 fusion.148
  100.6 0.5 convolution_bitcast_fusion.4
  101.1 0.5 fusion.149
  101.6 0.7 fusion.158
  102.8 0.5 convolution_subtract_fusion.3
  103.3 0.5 convolution_bitcast_fusion.5
  103.8 1.1 fusion.167
  104.9 106.5 %reduce-scatter.2.cloned.1.call-done = f32[288,128]{1,0:T(8,128)} async-done(((f32[9216,128]{1,0:T(8,128)}), f32[288,128]{1,0:T(8,128)}) %reduce-scatter.2.cloned.1.call-update) | async-done | bytes 147472 | tf_op jit(solution)/shard_map/reduce_scatter | solution.py:134
  211.4 1.7 fusion.61
  213.0 9.9 %all_gather.7 = bf16[2304,128]{1,0:T(8,128)(2,1)S(1)} all-gather(bf16[288,128]{1,0:T(8,128)(2,1)S(1)} %get-tuple-element.339), channel_id=1, replica_groups=mesh['section'=4,'dp'=8] {'dp'}, dimensions={0}, use_global_device_ids=true | all-gather | bytes 663552 | tf_op jit(solution)/shard_map/all_gather | solution.py:145
  223.0 0.8 copy.77
  (153 shorter events, 7.1 us)
Async XLA Ops:
  7.2 55.1 %all-gather.2.cloned.1.call-start = ((), (), s32[]{:S(2)}) async-start(), calls=%async_computation.1 | async-start | bytes 2949120 | tf_op jit(solution)/shard_map/all_gather | solution.py:97
  7.9 203.5 %reduce-scatter.2.cloned.1.call-start = ((), (), s32[]{:S(2)}) async-start(), calls=%async_computation.2 | async-start | bytes 4866048 | tf_op jit(solution)/shard_map/reduce_scatter | solution.py:134
  104.9 106.5 %copy-start = (f32[1,288,128]{2,1,0:T(8,128)S(1)}, f32[1,288,128]{2,1,0:T(8,128)}, u32[]{:S(2)}) copy-start(f32[1,288,128]{2,1,0:T(8,128)} %param.12) | copy-start | bytes 442372
  104.9 106.5 %copy-start.1 = (f32[1,288,128]{2,1,0:T(8,128)S(1)}, f32[1,288,128]{2,1,0:T(8,128)}, u32[]{:S(2)}) copy-start(f32[1,288,128]{2,1,0:T(8,128)} %param.13) | copy-start | bytes 442372
Sparse Core Ops, SparseCore 0:
  9.5 52.6 all-gather.1
  105.0 106.2 reduce-scatter.1
where the time goes:
time: 231 us
  waiting for transfers between devices  160 us (69%)
  local copies, waits for them, and re-layouts  20.2 us (9%)
  matrix products  16.9 us (7%)
  between operations  14.1 us (6%)
  blocking collectives  9.93 us (4%)
  other arithmetic  8.27 us (4%)
    reduce_scatter x1, waiting for transfers between devices, replicated_grads(): lax.psum_scatter(result[4].reshape(-1, channels), ('section', 'dp'), scat...  106 us
    all_gather x1, waiting for transfers between devices, replicated_grads(): gathered = lax.all_gather(weights, 'section', axis=0, tiled=True)  53.1 us
    all_gather x1, blocking collectives, on_device(): lax.all_gather(new_master.astype(jnp.bfloat16), 'dp', axis=0, tiled=True)  9.93 us
    dot_general x16, matrix products, convolve(): jnp.dot(patches, weight, preferred_element_type=jnp.float32)  9.05 us
    while x124, local copies, waits for them, and re-layouts  5.82 us
  transfers between devices with their start and end apart: 2, of which 2 were waited for; matrix products, arithmetic and copies ran while one was open for 1% of the time, Pallas kernels for 0%

commit v1 on v0

--- a/solution.py
+++ b/solution.py
@@ -94,7 +94,14 @@
     section_index = lax.axis_index("section")
     sections = lax.axis_size("section")
     channels = weights.shape[2]
-    gathered = lax.all_gather(weights, "section", axis=0, tiled=True)
+    ring = [weights]
+    for hop in range(3):
+        ring.append(lax.ppermute(ring[-1], "section", [(dev, (dev + 1) % 4) for dev in range(4)]))
+    gathered = jnp.roll(
+        jnp.concatenate(ring[::-1], axis=0),
+        (lax.axis_index("section") + 1) * ring[0].shape[0],
+        axis=0,
+    )
     all_blocks = gathered.reshape(sections, LAYERS, 2, 9 * channels, channels)
     share = stream.shape[1] // sections
     own = lax.dynamic_slice_in_dim(stream, section_index * share, share, 1)

time: 231 us -> 218 us (0.944)
  waiting for transfers between devices: 160 us -> 151 us
  local copies, waits for them, and re-layouts: 20.2 us -> 13.3 us
  starting transfers between devices: 0.08 us -> 3.15 us
    all_gather x1 -> x0, waiting for transfers between devices: 53.1 us -> none  [replicated_grads(): gathered = lax.all_gather(weights, 'section', axis=0, tiled=True)]
    ppermute x0 -> x3, waiting for transfers between devices: none -> 46 us  [replicated_grads(): lax.ppermute(ring[-1], 'section', [(dev, (dev + 1) % 4) for dev in range(...]
    squeeze x4, local copies, waits for them, and re-layouts: 4.44 us -> 0.19 us  [backward_one(): lax.dynamic_index_in_dim(all_blocks, section_idx, 0, keepdims=False)]
    squeeze x4, local copies, waits for them, and re-layouts: 4.44 us -> 0.19 us  [forward_one(): lax.dynamic_index_in_dim(all_blocks, section_idx, 0, keepdims=False)]
    ppermute x0 -> x3, starting transfers between devices: none -> 3.11 us  [replicated_grads(): lax.ppermute(ring[-1], 'section', [(dev, (dev + 1) % 4) for dev in range(...]
  transfers between devices with their start and end apart: 2 -> 4, of which waited for: 2 -> 4; matrix products, arithmetic and copies ran while one was open for 1% -> 1% of each run, Pallas kernels for 0% -> 0%
where the time goes in v1:
time: 218 us
  waiting for transfers between devices  151 us (69%)
  matrix products  16.9 us (8%)
  between operations  14.1 us (6%)
  local copies, waits for them, and re-layouts  13.3 us (6%)
  blocking collectives  10.1 us (5%)
  other arithmetic  8.27 us (4%)
  starting transfers between devices  3.15 us (1%)
    reduce_scatter x1, waiting for transfers between devices, replicated_grads(): lax.psum_scatter(result[4].reshape(-1, channels), ('section', 'dp'), scat...  105 us
    ppermute x3, waiting for transfers between devices, replicated_grads(): lax.ppermute(ring[-1], 'section', [(dev, (dev + 1) % 4) for dev in range(...  46 us
    all_gather x1, blocking collectives, on_device(): lax.all_gather(new_master.astype(jnp.bfloat16), 'dp', axis=0, tiled=True)  10.1 us
    dot_general x16, matrix products, convolve(): jnp.dot(patches, weight, preferred_element_type=jnp.float32)  9.06 us
    while x124, local copies, waits for them, and re-layouts  5.82 us
    dynamic_update_slice x4, other arithmetic, backward_one(): lax.dynamic_update_index_in_dim(grads, jnp.stack(pieces), section_idx, 0)  4.43 us
  transfers between devices with their start and end apart: 4, of which 4 were waited for; matrix products, arithmetic and copies ran while one was open for 1% of the time, Pallas kernels for 0%

profile of v1, /device:TPU:0, one launch (start us, length us, event | category | flops | bytes accessed | tf_op | source)
XLA Modules:
  0.0 218.2 jit_solution(8864133308226609178)
XLA Ops:
  7.2 3.1 %collective-permute-start = (bf16[1,2304,128]{2,1,0:T(8,128)(2,1)}, bf16[1,2304,128]{2,1,0:T(8,128)(2,1)S(1)}, u32[]{:S(2)}, u32[]{:S(2)}) collective-permute-start(bf16[1,2304,128]{2,1,0:T(8,128)(2,1)} %param.11), channel_id=1, source_target_pairs={{0,8},{8,16},{16,24},{24,0},{1,9},{9,17},{17,25},{25,1},{2,10},{10... | collective-permute-start | bytes 1769480 | tf_op jit(solution)/shard_map/ppermute | solution.py:99
  10.3 15.6 %collective-permute-done = bf16[1,2304,128]{2,1,0:T(8,128)(2,1)S(1)} collective-permute-done((bf16[1,2304,128]{2,1,0:T(8,128)(2,1)}, bf16[1,2304,128]{2,1,0:T(8,128)(2,1)S(1)}, u32[]{:S(2)}, u32[]{:S(2)}) %collective-permute-start) | collective-permute-done | bytes 589856 | tf_op jit(solution)/shard_map/ppermute | solution.py:99
  25.9 16.3 %collective-permute-done.1 = bf16[1,2304,128]{2,1,0:T(8,128)(2,1)S(1)} collective-permute-done((bf16[1,2304,128]{2,1,0:T(8,128)(2,1)S(1)}, bf16[1,2304,128]{2,1,0:T(8,128)(2,1)S(1)}, u32[]{:S(2)}, u32[]{:S(2)}) %collective-permute-start.1) | collective-permute-done | bytes 589856 | tf_op jit(solution)/shard_map/ppermute | solution.py:99
  42.2 1.3 dynamic-slice_bitcast_fusion.2
  43.4 14.2 %collective-permute-done.2 = bf16[1,2304,128]{2,1,0:T(8,128)(2,1)S(1)} collective-permute-done((bf16[1,2304,128]{2,1,0:T(8,128)(2,1)S(1)}, bf16[1,2304,128]{2,1,0:T(8,128)(2,1)S(1)}, u32[]{:S(2)}, u32[]{:S(2)}) %collective-permute-start.2) | collective-permute-done | bytes 589856 | tf_op jit(solution)/shard_map/ppermute | solution.py:99
  57.7 0.1 constant_dynamic-update-slice_fusion.10
  57.7 0.1 constant_dynamic-update-slice_fusion.9
  57.8 0.9 copy-done
  59.1 0.2 constant_dynamic-slice_fusion
  59.3 8.9 %while.40 = (s32[]{:T(128)}, f32[2,16,16,128]{3,2,1,0:T(8,128)S(1)}, f32[2,16,16,128]{3,2,1,0:T(8,128)S(1)}, bf16[4,1,2,1152,128]{4,3,2,1,0:T(8,128)(2,1)S(1)}, s32[]{:T(128)}) while((s32[]{:T(128)}, f32[2,16,16,128]{3,2,1,0:T(8,128)S(1)}, f32[2,16,16,128]{3,2,1,0:T(8,128)S(1)}, bf16[4,1,2,1152,128]{4,3,2,1,0:T(8,128)(2,1)S(1)}, ...), condition=%wide.region_1.2_spmd, body=%wide.region_0.1_spmd.sunk | while | flops 303104000 | bytes 10551369 | solution.py:118
  59.3 0.1 multiply_convert_fusion.6
  59.7 0.1 constant_dynamic-update-slice_fusion.16
  60.0 0.6 multiply_convert_fusion.7
  61.0 0.5 convolution_add_fusion.3
  61.5 0.1 multiply_convert_fusion.6
  61.9 0.1 constant_dynamic-update-slice_fusion.16
  62.2 0.6 multiply_convert_fusion.7
  63.3 0.5 convolution_add_fusion.3
  63.8 0.1 multiply_convert_fusion.6
  64.1 0.1 constant_dynamic-update-slice_fusion.16
  64.4 0.6 multiply_convert_fusion.7
  65.5 0.5 convolution_add_fusion.3
  66.0 0.1 multiply_convert_fusion.6
  66.3 0.1 constant_dynamic-update-slice_fusion.16
  66.7 0.6 multiply_convert_fusion.7
  67.7 0.5 convolution_add_fusion.3
  68.2 2.5 %broadcast_in_dim.23 = f32[4,1,2,1152,128]{4,3,2,1,0:T(8,128)} broadcast(f32[]{:T(128)} %constant.158.clone.1), dimensions={} | broadcast | bytes 4718596 | tf_op jit(solution)/shard_map/broadcast_in_dim | solution.py:139
  70.7 22.8 %while.41 = (s32[]{:T(128)}, f32[2,16,16,128]{3,2,1,0:T(8,128)S(1)}, f32[2,16,16,128]{3,2,1,0:T(8,128)S(1)}, f32[2,16,16,128]{3,2,1,0:T(8,128)S(1)}, f32[2,16,16...) while((s32[]{:T(128)}, ...), condition=%wide.region_3.4_spmd, body=%wide.region_2.3_spmd.sunk | while | flops 909082624 | bytes 29098156 | solution.py:140
  70.8 0.5 fusion.147
  71.3 0.3 fusion.148
  72.1 0.5 convolution_bitcast_fusion.4
  72.6 0.5 fusion.149
  73.1 0.7 fusion.158
  74.3 0.5 convolution_subtract_fusion.3
  74.8 0.5 convolution_bitcast_fusion.5
  75.3 1.1 fusion.167
  76.5 0.5 fusion.147
  77.0 0.3 fusion.148
  77.8 0.5 convolution_bitcast_fusion.4
  78.3 0.5 fusion.149
  78.8 0.7 fusion.158
  80.0 0.5 convolution_subtract_fusion.3
  80.5 0.5 convolution_bitcast_fusion.5
  81.0 1.1 fusion.167
  82.2 0.5 fusion.147
  82.7 0.3 fusion.148
  83.5 0.5 convolution_bitcast_fusion.4
  84.0 0.5 fusion.149
  84.5 0.7 fusion.158
  85.7 0.5 convolution_subtract_fusion.3
  86.2 0.5 convolution_bitcast_fusion.5
  86.7 1.1 fusion.167
  87.9 0.5 fusion.147
  88.3 0.3 fusion.148
  89.2 0.5 convolution_bitcast_fusion.4
  89.7 0.5 fusion.149
  90.2 0.7 fusion.158
  91.4 0.5 convolution_subtract_fusion.3
  91.9 0.5 convolution_bitcast_fusion.5
  92.4 1.1 fusion.167
  93.5 105.2 %reduce-scatter.2.cloned.1.call-done = f32[288,128]{1,0:T(8,128)} async-done(((f32[9216,128]{1,0:T(8,128)}), f32[288,128]{1,0:T(8,128)}) %reduce-scatter.2.cloned.1.call-update) | async-done | bytes 147472 | tf_op jit(solution)/shard_map/reduce_scatter | solution.py:141
  198.7 1.7 fusion.61
  200.4 10.1 %all_gather.3 = bf16[2304,128]{1,0:T(8,128)(2,1)S(1)} all-gather(bf16[288,128]{1,0:T(8,128)(2,1)S(1)} %get-tuple-element.328), channel_id=1, replica_groups=mesh['section'=4,'dp'=8] {'dp'}, dimensions={0}, use_global_device_ids=true | all-gather | bytes 663552 | tf_op jit(solution)/shard_map/all_gather | solution.py:152
  210.5 0.8 copy.82
  (167 shorter events, 7.7 us)
Async XLA Ops:
  7.2 191.6 %reduce-scatter.2.cloned.1.call-start = ((), (), s32[]{:S(2)}) async-start(), calls=%async_computation.1 | async-start | bytes 4866048 | tf_op jit(solution)/shard_map/reduce_scatter | solution.py:141
  7.2 18.7 %collective-permute-start = (bf16[1,2304,128]{2,1,0:T(8,128)(2,1)}, bf16[1,2304,128]{2,1,0:T(8,128)(2,1)S(1)}, u32[]{:S(2)}, u32[]{:S(2)}) collective-permute-start(bf16[1,2304,128]{2,1,0:T(8,128)(2,1)} %param.11), channel_id=1, source_target_pairs={{0,8},{8,16},{16,24},{24,0},{1,9},{9,17},{17,25},{25,1},{2,10},{10... | collective-permute-start | bytes 1769480 | tf_op jit(solution)/shard_map/ppermute | solution.py:99
  25.9 16.3 %collective-permute-start.1 = (bf16[1,2304,128]{2,1,0:T(8,128)(2,1)S(1)}, bf16[1,2304,128]{2,1,0:T(8,128)(2,1)S(1)}, u32[]{:S(2)}, u32[]{:S(2)}) collective-permute-start(bf16[1,2304,128]{2,1,0:T(8,128)(2,1)S(1)} %collective-permute-done), channel_id=1, source_target_pairs={{0,8},{8,16},{16,24},{24,0},{1,9},{9,17},{17,25},{25,1},{2,10},{10... | collective-permute-start | bytes 1769480 | tf_op jit(solution)/shard_map/ppermute | solution.py:99
  42.2 15.4 %collective-permute-start.2 = (bf16[1,2304,128]{2,1,0:T(8,128)(2,1)S(1)}, bf16[1,2304,128]{2,1,0:T(8,128)(2,1)S(1)}, u32[]{:S(2)}, u32[]{:S(2)}) collective-permute-start(bf16[1,2304,128]{2,1,0:T(8,128)(2,1)S(1)} %collective-permute-done.1), channel_id=1, source_target_pairs={{0,8},{8,16},{16,24},{24,0},{1,9},{9,17},{17,25},{25,1},{2,10},{10... | collective-permute-start | bytes 1769480 | tf_op jit(solution)/shard_map/ppermute | solution.py:99
  57.6 1.1 copy-start
  93.5 105.3 %copy-start.1 = (f32[1,288,128]{2,1,0:T(8,128)S(1)}, f32[1,288,128]{2,1,0:T(8,128)}, u32[]{:S(2)}) copy-start(f32[1,288,128]{2,1,0:T(8,128)} %param.12) | copy-start | bytes 442372
  93.5 105.3 %copy-start.2 = (f32[1,288,128]{2,1,0:T(8,128)S(1)}, f32[1,288,128]{2,1,0:T(8,128)}, u32[]{:S(2)}) copy-start(f32[1,288,128]{2,1,0:T(8,128)} %param.13) | copy-start | bytes 442372
Sparse Core Ops, SparseCore 0:
  93.6 105.0 reduce-scatter.1
